TPU v7x, 512 devices: a whole 4x8x8 slice. The times are simulated.
512 devices in a mesh: resp: 64 (over y, z), head: 8 (over x, core).
Axes of the slice: x: 4, y: 8, z: 8, core: 2. Of those that a mesh axis runs over, the one named last changes fastest.
Arguments:
- queries: bfloat16 [8192, 24576], P('resp', 'head'), may hold values from -8 to 8
- resp_latent: bfloat16 [8192, 576], P('resp'), may hold values from -8 to 8
- prompt_latent: bfloat16 [64, 128, 576], P('resp'), may hold values from -6 to 6
- up_keys: bfloat16 [128, 128, 512], P('head', None, 'resp'), may hold values from -0.5 to 0.5
- up_values: bfloat16 [128, 512, 128], P('head', 'resp'), may hold values from -0.25 to 0.25
- cotangent: bfloat16 [8192, 16384], P('resp', 'head'), may hold values from -6 to 6
- prompt_len: int32 [32], replicated, may hold values from 32 to 128
- resp_len: int32 [128], replicated, may hold values from 16 to 64
- resp_count: int32 [32], replicated, may hold values from 1 to 8, 128 in all
- owner: int32 [32], replicated, may hold values from 0 to 63, as said below
Outputs:
- attended: bfloat16 [8192, 16384], P('resp', 'head')
- grad_queries: bfloat16 [8192, 24576], P('resp', 'head')
- grad_response: float32 [8192, 576], P('resp', 'head')
- grad_prompt: float32 [64, 128, 576], P('resp', None, 'head')
Inputs may be any that keep to these rules, and one draw needn't show every extreme that they name: Distinct slots; prompt p's cache is prompt_latent[owner[p]]. `resp_count`: every prompt has at least one response; they sum to 128.
All inputs are finite; a program needn't handle non-finite values.
Results may differ from a plain program's by a relative error of at most 0.014.
Values may be sent and summed in bfloat16 or wider, within the bound.
No kernel may reach another device: no remote copies, remote signals or barrier semaphores. Data moves between devices by JAX's collectives and lax.ppermute only.
A program may use at most 64 MiB of HBM per device.

v0:
```python
import math
import jax
import jax.numpy as jnp
from jax import lax
from jax.sharding import PartitionSpec as P


def turned_gather(arrays, axis, dims):
    turned = [jnp.moveaxis(a, dim, 0) for a, dim in zip(arrays, dims)]
    both = jnp.concatenate([t.reshape(len(t), -1) for t in turned], axis=1)
    out, at, done = (lax.all_gather(both, axis, axis=0, tiled=True), 0, [])
    for t, dim in zip(turned, dims):
        piece = out[:, at : at + t[0].size].reshape(-1, *t.shape[1:])
        done.append(jnp.moveaxis(piece, 0, dim))
        at += t[0].size
    return tuple(done)


def in_order(tiles, dim):
    tiles = jnp.moveaxis(tiles, 0, dim)
    lengths = tiles.shape
    return tiles.reshape(*lengths[:dim], lengths[dim] * lengths[dim + 1], *lengths[dim + 2 :])


def sent_to_all(array, axis):
    copies = jnp.broadcast_to(array, (lax.axis_size(axis), *array.shape))
    return lax.all_to_all(copies, axis, split_axis=0, concat_axis=0, tiled=True)


def gathered_copies(array, axis, dim):
    return in_order(sent_to_all(array, axis), dim)


def split_up(array, dim, length):
    before, after = (array.shape[:dim], array.shape[dim + 1 :])
    return jnp.moveaxis(array.reshape(*before, length, -1, *after), dim, 0)


def sent_and_summed(array, axis, dim):
    length = lax.axis_size(axis)
    tiles = lax.all_to_all(split_up(array, dim, length), axis, 0, 0, tiled=True)
    return jnp.sum(tiles.astype(jnp.float32), axis=0)


def product(form, left, right):
    return jnp.einsum(form, left, right, preferred_element_type=jnp.float32)


def attend(queries, key_rows, key_valid, row_live, cotangent, up_keys, up_values):
    head_count, nope_width, latent_width = up_keys.shape
    row_count = queries.shape[0]
    split_query = queries.reshape(row_count, head_count, -1)
    score_scale = 1.0 / math.sqrt(split_query.shape[2])
    query_latent = product("thn,hnc->thc", split_query[:, :, :nope_width], up_keys).astype(
        jnp.bfloat16
    )
    query_full = jnp.concatenate([query_latent, split_query[:, :, nope_width:]], axis=2)
    scores = product("thc,kc->thk", query_full, key_rows) * score_scale
    scores = jnp.where(key_valid[:, None, :], scores, -jnp.inf)
    row_max = jnp.max(scores, axis=2, keepdims=True)
    expo = jnp.exp(scores - row_max)
    weights = expo / jnp.sum(expo, axis=2, keepdims=True)
    weights_bf = weights.astype(jnp.bfloat16)
    value_rows = key_rows[:, :latent_width]
    latent_out = product("thk,kc->thc", weights_bf, value_rows).astype(jnp.bfloat16)
    attended = product("thc,hcv->thv", latent_out, up_values) * row_live[:, None, None]
    grad_out = cotangent.reshape(row_count, head_count, -1)
    grad_latent = (product("thv,hcv->thc", grad_out, up_values) * row_live[:, None, None]).astype(
        jnp.bfloat16
    )
    grad_weights = product("thc,kc->thk", grad_latent, value_rows)
    inner = jnp.sum(weights * grad_weights, axis=2, keepdims=True)
    grad_scores = (weights * (grad_weights - inner) * score_scale).astype(jnp.bfloat16)
    grad_full = product("thk,kc->thc", grad_scores, key_rows)
    grad_nope = product(
        "thc,hnc->thn", grad_full[:, :, :latent_width].astype(jnp.bfloat16), up_keys
    )
    grad_query = jnp.concatenate([grad_nope, grad_full[:, :, latent_width:]], axis=2)
    grad_key = product("thk,thc->kc", grad_scores, query_full)
    grad_value = product("thk,thc->kc", weights_bf, grad_latent)
    grad_key = grad_key + jnp.pad(grad_value, ((0, 0), (0, key_rows.shape[1] - latent_width)))
    return (
        attended.reshape(row_count, -1).astype(jnp.bfloat16),
        grad_query.reshape(row_count, -1).astype(jnp.bfloat16),
        grad_key,
    )


def body(
    queries,
    resp_latent,
    prompt_latent,
    up_keys,
    up_values,
    cotangent,
    prompt_len,
    resp_len,
    resp_count,
    owner,
):
    resp_devices = lax.axis_size("resp")
    head_devices = lax.axis_size("head")
    my_index = lax.axis_index("resp")
    head_index = lax.axis_index("head")
    keys_full, values_full = turned_gather((up_keys, up_values), "resp", (2, 1))
    resp_total = resp_len.shape[0]
    per_device = resp_total // resp_devices
    row_count = queries.shape[0] // per_device
    prompt_rows = prompt_latent.shape[1]
    piece_rows = prompt_rows // resp_devices
    latent_cols = prompt_latent.shape[2]
    starts = jnp.cumsum(resp_count) - resp_count
    numbers = jnp.arange(resp_total, dtype=jnp.int32)
    prompt_of = jnp.sum((starts[None, :] <= numbers[:, None]).astype(jnp.int32), axis=1) - 1
    chosen = prompt_of[:, None] == jnp.arange(prompt_len.shape[0], dtype=jnp.int32)[None, :]
    slot_of = jnp.sum(jnp.where(chosen, owner[None, :], 0), axis=1)
    plen_of = jnp.sum(jnp.where(chosen, prompt_len[None, :], 0), axis=1)
    plen_mine = lax.dynamic_slice_in_dim(plen_of, my_index * per_device, per_device)
    rlen_mine = lax.dynamic_slice_in_dim(resp_len, my_index * per_device, per_device)
    col_share = latent_cols // head_devices
    latent_share = lax.dynamic_slice_in_dim(prompt_latent, head_index * col_share, col_share, 2)
    stripes = lax.all_to_all(latent_share, "resp", split_axis=1, concat_axis=0, tiled=True)
    outgoing = jnp.take(stripes, slot_of, axis=0)
    outgoing = outgoing.reshape(resp_devices, per_device, piece_rows, stripes.shape[2])
    fetched = lax.all_to_all(outgoing, "resp", split_axis=0, concat_axis=2, tiled=True)[0]
    fetched = gathered_copies(fetched, "head", 2)
    own_rows = resp_latent.reshape(per_device, row_count, latent_cols)
    key_rows = jnp.concatenate([fetched, own_rows], axis=1)
    positions = jnp.arange(row_count, dtype=jnp.int32)
    prompt_pos = jnp.arange(prompt_rows, dtype=jnp.int32)
    prompt_ok = jnp.broadcast_to(
        prompt_pos[None, None, :] < plen_mine[:, None, None], (per_device, row_count, prompt_rows)
    )
    causal = jnp.broadcast_to(
        positions[None, :, None] >= positions[None, None, :], (per_device, row_count, row_count)
    )
    key_valid = jnp.concatenate([prompt_ok, causal], axis=2)
    row_live = (positions[None, :] < rlen_mine[:, None]).astype(jnp.float32)
    query_blocks = queries.reshape(per_device, row_count, -1)
    grad_blocks = cotangent.reshape(per_device, row_count, -1)
    attended, grad_query, grad_key = jax.vmap(attend, in_axes=(0, 0, 0, 0, 0, None, None))(
        query_blocks, key_rows, key_valid, row_live, grad_blocks, keys_full, values_full
    )
    grad_prompt_rows = grad_key[:, :prompt_rows]
    grad_own = grad_key[:, prompt_rows:].reshape(per_device * row_count, latent_cols)
    grad_prompt_rows, grad_own = (
        sent_and_summed(grad_prompt_rows.astype(jnp.bfloat16), "head", 2),
        sent_and_summed(grad_own.astype(jnp.bfloat16), "head", 1),
    )
    sent_cols = grad_prompt_rows.shape[2]
    arrived = lax.all_to_all(
        grad_prompt_rows[None].astype(jnp.bfloat16), "resp", split_axis=2, concat_axis=0, tiled=True
    ).astype(jnp.float32)
    flat_rows = arrived.reshape(resp_devices * per_device, piece_rows * sent_cols)
    slot_table = (slot_of[None, :] == jnp.arange(resp_devices, dtype=jnp.int32)[:, None]).astype(
        jnp.float32
    )
    summed = jnp.dot(slot_table, flat_rows, precision=lax.Precision.HIGHEST)
    summed = summed.reshape(resp_devices, piece_rows, sent_cols)
    at_owner = lax.all_to_all(
        summed.astype(jnp.bfloat16), "resp", split_axis=0, concat_axis=1, tiled=True
    ).astype(summed.dtype)
    return (
        attended.reshape(per_device * row_count, -1),
        grad_query.reshape(per_device * row_count, -1),
        grad_own,
        at_owner,
    )


def solution(mesh):
    placed = (
        P("resp", "head"),
        P("resp", None),
        P("resp", None, None),
        P("head", None, "resp"),
        P("head", "resp", None),
        P("resp", "head"),
        P(),
        P(),
        P(),
        P(),
    )
    return jax.shard_map(
        body,
        mesh=mesh,
        in_specs=placed,
        out_specs=(
            P("resp", "head"),
            P("resp", "head"),
            P("resp", "head"),
            P("resp", None, "head"),
        ),
        check_vma=False,
    )
```

profile of v0, /device:TPU:1, one launch (start us, length us, event | category | flops | bytes accessed | tf_op | source)
XLA Modules:
  0.0 217.1 jit_solution(1038570056481774946)
XLA Ops:
  7.2 1.5 pad_maximum_fusion.3
  8.8 0.8 copy.159
  9.5 17.1 %all-to-all-start = ((bf16[1,128,72]{2,0,1:T(2,128)(2,1)}), bf16[1,128,72]{2,0,1:T(2,128)(2,1)S(1)}, u32[]{:S(2)}, u32[]{:S(2)}) async-start(bf16[1,128,72]{2,0,1:T(2,128)(2,1)} %copy.159), calls=%async_computation | async-start | bytes 131072 | tf_op jit(solution)/shard_map/all_to_all | solution.py:122
  26.7 0.7 copy.118
  28.3 0.8 select_reduce_fusion.1
  29.4 8.4 %all-to-all-done = bf16[1,128,72]{2,0,1:T(2,128)(2,1)S(1)} async-done(((bf16[1,128,72]{2,0,1:T(2,128)(2,1)}), bf16[1,128,72]{2,0,1:T(2,128)(2,1)S(1)}, u32[]{:S(2)}, u32[]{:S(2)}) %all-to-all-start) | async-done | bytes 18464 | tf_op jit(solution)/shard_map/all_to_all | solution.py:122
  37.8 0.7 gather_fusion
  38.5 0.8 broadcast_select_fusion
  39.4 4.6 %all-to-all-start.1 = ((bf16[64,2,2,72]{3,2,1,0:T(2,128)(2,1)}), bf16[64,2,2,72]{3,2,1,0:T(2,128)(2,1)S(1)}, u32[]{:S(2)}, u32[]{:S(2)}) async-start(bf16[64,2,2,72]{3,2,1,0:T(2,128)(2,1)} %broadcast_select_fusion), calls=%async_computation.1 | async-start | bytes 131072 | tf_op jit(solution)/shard_map/all_to_all | solution.py:125
  44.0 11.2 %all-to-all-done.1 = bf16[64,2,2,72]{3,2,1,0:T(2,128)(2,1)S(1)} async-done(((bf16[64,2,2,72]{3,2,1,0:T(2,128)(2,1)}), bf16[64,2,2,72]{3,2,1,0:T(2,128)(2,1)S(1)}, u32[]{:S(2)}, u32[]{:S(2)}) %all-to-all-start.1) | async-done | bytes 36896 | tf_op jit(solution)/shard_map/all_to_all | solution.py:125
  55.4 0.8 broadcast_in_dim.82
  56.1 7.5 %all-to-all-start.2 = ((bf16[8,2,128,72]{2,3,1,0:T(8,128)(2,1)}), bf16[8,2,128,72]{2,3,1,0:T(8,128)(2,1)}, u32[]{:S(2)}, u32[]{:S(2)}) async-start(bf16[8,2,128,72]{2,3,1,0:T(8,128)(2,1)} %broadcast_in_dim.82), calls=%async_computation.2 | async-start | bytes 589824 | tf_op jit(solution)/shard_map/all_to_all | solution.py:27
  63.7 1.1 reshape_reshape.6
  65.7 0.9 copy.160
  66.7 3.8 %all-to-all-done.2 = bf16[8,2,128,72]{2,3,1,0:T(8,128)(2,1)} async-done(((bf16[8,2,128,72]{2,3,1,0:T(8,128)(2,1)}), bf16[8,2,128,72]{2,3,1,0:T(8,128)(2,1)}, u32[]{:S(2)}, u32[]{:S(2)}) %all-to-all-start.2) | async-done | bytes 294944 | tf_op jit(solution)/shard_map/all_to_all | solution.py:27
  70.5 1.0 copy.125
  71.5 0.9 copy.127
  72.4 26.7 %all-gather.2.cloned.1.call-done = bf16[512,4096]{1,0:T(8,128)(2,1)} async-done(((bf16[8,4096]{1,0:T(8,128)(2,1)}), bf16[512,4096]{1,0:T(8,128)(2,1)}) %all-gather.2.cloned.1.call-update) | async-done | bytes 4194320 | tf_op jit(solution)/shard_map/all_gather | solution.py:11
  99.2 4.8 %fusion.55 = (bf16[512,2048]{1,0:T(8,128)(2,1)}, bf16[512,2048]{1,0:T(8,128)(2,1)}) fusion(bf16[512,4096]{1,0:T(8,128)(2,1)} %all-gather.2.cloned.1.call-done), kind=kLoop, calls=%fused_computation.79 | loop fusion | bytes 8388608 | tf_op jit(solution)/shard_map/slice | solution.py:13
  104.0 2.9 %copy.116 = bf16[512,2048]{0,1:T(8,128)(2,1)S(1)} copy(bf16[512,2048]{1,0:T(8,128)(2,1)} %get-tuple-element.22) | data formatting | bytes 4194304 | tf_op jit(solution)/shard_map/slice | solution.py:13
  106.8 2.4 %copy.117 = bf16[512,16,128]{2,0,1:T(8,128)(2,1)} copy(bf16[512,16,128]{0,2,1:T(8,128)(2,1)S(1)} %bitcast.123) | data formatting | bytes 4194304 | tf_op jit(solution)/shard_map/reshape | solution.py:13
  109.3 2.9 %copy.119 = bf16[512,2048]{0,1:T(8,128)(2,1)S(1)} copy(bf16[512,2048]{1,0:T(8,128)(2,1)} %get-tuple-element.23) | data formatting | bytes 4194304 | tf_op jit(solution)/shard_map/slice | solution.py:13
  112.1 1.7 fusion.66
  114.2 1.9 pad_maximum_fusion
  116.1 5.2 %fusion.56 = (f32[2,64,16]{2,1,0:T(8,128)S(1)}, f32[2,64,16,192]{3,2,1,0:T(8,128)}) fusion(pred[2,64,192]{2,1,0:T(8,128)(4,1)S(1)} %pad_add_fusion, bf16[2,64,16,576]{3,1,0,2:T(8,128)(2,1)} %pad_maximum_fusion, bf16[2,64,576]{2,1,0:T(8,128)(2,1)S(1)} %bitcast.134, bf16[2,128,576]{2,1,0:T(8,128)(2,1)} %copy.127), kind=kOutput, calls=%fused_computation.80 | convolution fusion | flops 455442624 | bytes 4407296 | tf_op jit(solution)/shard_map/vmap()/sub | solution.py:61
  121.3 2.0 fusion.54
  123.3 0.7 convolution_convert_fusion.1
  124.0 0.9 copy-done.1
  126.3 0.7 fusion.22
  127.0 1.3 fusion.13
  128.6 11.3 %multiply_convert_fusion.1 = bf16[2,64,16,192]{3,2,1,0:T(8,128)(2,1)S(1)} fusion(f32[2,64,16,192]{3,2,1,0:T(8,128)S(1)} %fusion.13, f32[2,64,16,192]{3,2,1,0:T(8,128)S(1)} %copy-done.4, f32[2,64,16]{2,1,0:T(8,128)S(1)} %get-tuple-element.24), kind=kOutput, calls=%fused_computation.18 | output fusion | flops 2754751 | bytes 3940352 | tf_op jit(solution)/shard_map/vmap()/sub | solution.py:73
  139.9 0.9 fusion.28
  140.8 1.0 convolution_convert_fusion
  141.8 1.8 slice.48
  145.3 0.9 copy.191
  146.4 0.8 copy.143
  147.2 9.1 %all-to-all-start.4 = ((bf16[8,2,128,72]{2,3,1,0:T(8,128)(2,1)}), bf16[8,2,128,72]{2,3,1,0:T(8,128)(2,1)S(1)}, u32[]{:S(2)}, u32[]{:S(2)}) async-start(bf16[8,2,128,72]{2,3,1,0:T(8,128)(2,1)} %copy.143), calls=%async_computation.4 | async-start | bytes 589824 | tf_op jit(solution)/shard_map/all_to_all | solution.py:41
  156.6 0.8 copy.140
  157.4 2.8 %copy.133 = bf16[2,64,16,512]{3,1,0,2:T(8,128)(2,1)S(1)} copy(bf16[2,64,16,512]{3,2,1,0:T(8,128)(2,1)} %slice.48) | data formatting | bytes 4194304 | tf_op jit(solution)/shard_map/vmap()/slice | solution.py:76
  161.4 1.6 all-to-all-done.4
  163.1 0.7 copy.145
  163.8 8.0 %all-to-all-start.5 = ((bf16[1,2,128,72]{3,1,0,2:T(2,128)(2,1)}), bf16[1,2,128,72]{3,1,0,2:T(2,128)(2,1)S(1)}, u32[]{:S(2)}, u32[]{:S(2)}) async-start(bf16[1,2,128,72]{3,1,0,2:T(2,128)(2,1)} %copy.145), calls=%async_computation.5 | async-start | bytes 131072 | tf_op jit(solution)/shard_map/all_to_all | solution.py:151
  172.7 2.0 convert_element_type.102
  174.7 8.3 %all-to-all-done.5 = bf16[1,2,128,72]{3,1,0,2:T(2,128)(2,1)S(1)} async-done(((bf16[1,2,128,72]{3,1,0,2:T(2,128)(2,1)}), bf16[1,2,128,72]{3,1,0,2:T(2,128)(2,1)S(1)}, u32[]{:S(2)}, u32[]{:S(2)}) %all-to-all-start.5) | async-done | bytes 36896 | tf_op jit(solution)/shard_map/all_to_all | solution.py:151
  183.0 5.8 %all-to-all-start.3 = ((bf16[8,128,72]{1,2,0:T(8,128)(2,1)}), bf16[8,128,72]{1,2,0:T(8,128)(2,1)S(1)}, u32[]{:S(2)}, u32[]{:S(2)}) async-start(bf16[8,128,72]{1,2,0:T(8,128)(2,1)} %copy.140), calls=%async_computation.3 | async-start | bytes 294912 | tf_op jit(solution)/shard_map/all_to_all | solution.py:41
  189.9 4.3 %all-to-all-done.3 = bf16[8,128,72]{1,2,0:T(8,128)(2,1)S(1)} async-done(((bf16[8,128,72]{1,2,0:T(8,128)(2,1)}), bf16[8,128,72]{1,2,0:T(8,128)(2,1)S(1)}, u32[]{:S(2)}, u32[]{:S(2)}) %all-to-all-start.3) | async-done | bytes 147488 | tf_op jit(solution)/shard_map/all_to_all | solution.py:41
  194.2 4.6 %all-to-all-start.6 = ((bf16[64,2,72]{2,1,0:T(2,128)(2,1)}), bf16[64,2,72]{2,1,0:T(2,128)(2,1)S(1)}, u32[]{:S(2)}, u32[]{:S(2)}) async-start(bf16[64,2,72]{2,1,0:T(2,128)(2,1)} %copy.149), calls=%async_computation.6 | async-start | bytes 65536 | tf_op jit(solution)/shard_map/all_to_all | solution.py:160
  199.5 10.1 %all-to-all-done.6 = bf16[64,2,72]{2,1,0:T(2,128)(2,1)S(1)} async-done(((bf16[64,2,72]{2,1,0:T(2,128)(2,1)}), bf16[64,2,72]{2,1,0:T(2,128)(2,1)S(1)}, u32[]{:S(2)}, u32[]{:S(2)}) %all-to-all-start.6) | async-done | bytes 18464 | tf_op jit(solution)/shard_map/all_to_all | solution.py:160
  (79 shorter events, 11.1 us)
Async XLA Ops:
  7.2 1.6 copy-start
  7.2 56.5 %copy-start.7 = (bf16[128,3072]{1,0:T(8,128)(2,1)S(1)}, bf16[128,3072]{1,0:T(8,128)(2,1)}, u32[]{:S(2)}) copy-start(bf16[128,3072]{1,0:T(8,128)(2,1)} %param.10) | copy-start | bytes 2359300
  7.2 92.0 %all-gather.2.cloned.1.call-start = ((), (), s32[]{:S(2)}) async-start(), calls=%async_computation.7 | async-start | bytes 4259840 | tf_op jit(solution)/shard_map/all_gather | solution.py:11
  9.5 28.3 %all-to-all-start = ((bf16[1,128,72]{2,0,1:T(2,128)(2,1)}), bf16[1,128,72]{2,0,1:T(2,128)(2,1)S(1)}, u32[]{:S(2)}, u32[]{:S(2)}) async-start(bf16[1,128,72]{2,0,1:T(2,128)(2,1)} %copy.159), calls=%async_computation | async-start | bytes 131072 | tf_op jit(solution)/shard_map/all_to_all | solution.py:122
  39.4 15.9 %all-to-all-start.1 = ((bf16[64,2,2,72]{3,2,1,0:T(2,128)(2,1)}), bf16[64,2,2,72]{3,2,1,0:T(2,128)(2,1)S(1)}, u32[]{:S(2)}, u32[]{:S(2)}) async-start(bf16[64,2,2,72]{3,2,1,0:T(2,128)(2,1)} %broadcast_select_fusion), calls=%async_computation.1 | async-start | bytes 131072 | tf_op jit(solution)/shard_map/all_to_all | solution.py:125
  56.1 14.4 %all-to-all-start.2 = ((bf16[8,2,128,72]{2,3,1,0:T(8,128)(2,1)}), bf16[8,2,128,72]{2,3,1,0:T(8,128)(2,1)}, u32[]{:S(2)}, u32[]{:S(2)}) async-start(bf16[8,2,128,72]{2,3,1,0:T(8,128)(2,1)} %broadcast_in_dim.82), calls=%async_computation.2 | async-start | bytes 589824 | tf_op jit(solution)/shard_map/all_to_all | solution.py:27
  63.6 1.4 copy-start.10
  63.6 1.5 copy-start.9
  63.7 1.6 copy-start.8
  121.3 2.0 copy-start.5
  123.3 1.6 copy-start.1
  127.0 1.6 copy-start.4
  128.6 11.3 %copy-start.3 = (bf16[2,64,16,576]{3,1,0,2:T(8,128)(2,1)S(1)}, bf16[2,64,16,576]{3,1,0,2:T(8,128)(2,1)}, u32[]{:S(2)}) copy-start(bf16[2,64,16,576]{3,1,0,2:T(8,128)(2,1)} %pad_maximum_fusion) | copy-start | bytes 7077892
  140.8 1.0 copy-start.6
  141.8 2.2 copy-start.2
  144.7 1.5 slice-start.2
  144.9 11.4 %slice-start.1 = ((bf16[2,192,576]{2,1,0:T(8,128)(2,1)}), bf16[2,64,576]{2,1,0:T(8,128)(2,1)S(1)}, s32[]{:S(2)}) async-start(bf16[2,192,576]{2,1,0:T(8,128)(2,1)} %copy-done.6), calls=%async_computation.9 | async-start | bytes 327680 | tf_op jit(solution)/shard_map/slice | solution.py:145
  147.2 15.9 %all-to-all-start.4 = ((bf16[8,2,128,72]{2,3,1,0:T(8,128)(2,1)}), bf16[8,2,128,72]{2,3,1,0:T(8,128)(2,1)S(1)}, u32[]{:S(2)}, u32[]{:S(2)}) async-start(bf16[8,2,128,72]{2,3,1,0:T(8,128)(2,1)} %copy.143), calls=%async_computation.4 | async-start | bytes 589824 | tf_op jit(solution)/shard_map/all_to_all | solution.py:41
  160.1 1.0 slice-start
  163.8 19.2 %all-to-all-start.5 = ((bf16[1,2,128,72]{3,1,0,2:T(2,128)(2,1)}), bf16[1,2,128,72]{3,1,0,2:T(2,128)(2,1)S(1)}, u32[]{:S(2)}, u32[]{:S(2)}) async-start(bf16[1,2,128,72]{3,1,0,2:T(2,128)(2,1)} %copy.145), calls=%async_computation.5 | async-start | bytes 131072 | tf_op jit(solution)/shard_map/all_to_all | solution.py:151
  183.0 11.2 %all-to-all-start.3 = ((bf16[8,128,72]{1,2,0:T(8,128)(2,1)}), bf16[8,128,72]{1,2,0:T(8,128)(2,1)S(1)}, u32[]{:S(2)}, u32[]{:S(2)}) async-start(bf16[8,128,72]{1,2,0:T(8,128)(2,1)} %copy.140), calls=%async_computation.3 | async-start | bytes 294912 | tf_op jit(solution)/shard_map/all_to_all | solution.py:41
  194.2 15.4 %all-to-all-start.6 = ((bf16[64,2,72]{2,1,0:T(2,128)(2,1)}), bf16[64,2,72]{2,1,0:T(2,128)(2,1)S(1)}, u32[]{:S(2)}, u32[]{:S(2)}) async-start(bf16[64,2,72]{2,1,0:T(2,128)(2,1)} %copy.149), calls=%async_computation.6 | async-start | bytes 65536 | tf_op jit(solution)/shard_map/all_to_all | solution.py:160
Sparse Core Ops, SparseCore 0:
  11.0 88.1 all-gather.1
where the time goes:
time: 218 us; the launch traced here: 217 us
  waiting for transfers between devices  74.4 us (34%)
  starting transfers between devices  56.8 us (26%)
  local copies, waits for them, and re-layouts  36.1 us (17%)
  other arithmetic  21.5 us (10%)
  between operations  14.5 us (7%)
  matrix products  13.8 us (6%)
    all_gather x1, waiting for transfers between devices, turned_gather(): out, at, done = (lax.all_gather(both, axis, axis=0, tiled=True), 0, [])  26.7 us
    all_to_all x1, starting transfers between devices, body(): lax.all_to_all(latent_share, 'resp', split_axis=1, concat_axis=0, tiled=T...  17.1 us
    all_to_all x2, starting transfers between devices, sent_and_summed(): tiles = lax.all_to_all(split_up(array, dim, length), axis, 0, 0, tiled=True)  14.9 us
    sub x1, other arithmetic, attend(): grad_weights - inner  11.3 us
    all_to_all x1, waiting for transfers between devices, body(): lax.all_to_all(outgoing, 'resp', split_axis=0, concat_axis=2, tiled=True)[0]  11.2 us
    slice x3, local copies, waits for them, and re-layouts, turned_gather(): piece = out[:, at:at + t[0].size].reshape(-1, *t.shape[1:])  10.5 us
    all_to_all x1, waiting for transfers between devices, body(): lax.all_to_all(summed.astype(jnp.bfloat16), 'resp', split_axis=0, concat_...  10.1 us
    all_to_all x1, waiting for transfers between devices, body(): lax.all_to_all(latent_share, 'resp', split_axis=1, concat_axis=0, tiled=T...  8.36 us
  transfers between devices with their start and end apart: 8, of which 8 were waited for; matrix products, arithmetic and copies ran while one was open for 9% of the time, Pallas kernels for 0%

commit v1 on v0

--- a/solution.py
+++ b/solution.py
@@ -5,10 +5,17 @@
 from jax.sharding import PartitionSpec as P
 
 
+def all_by_exchange(x, mesh_axis, dim):
+    n_dev = lax.axis_size(mesh_axis)
+    blocks = jnp.stack([x for _ in range(n_dev)])
+    blocks = lax.all_to_all(blocks, mesh_axis, split_axis=0, concat_axis=0)
+    return jnp.concatenate(blocks, axis=dim)
+
+
 def turned_gather(arrays, axis, dims):
     turned = [jnp.moveaxis(a, dim, 0) for a, dim in zip(arrays, dims)]
     both = jnp.concatenate([t.reshape(len(t), -1) for t in turned], axis=1)
-    out, at, done = (lax.all_gather(both, axis, axis=0, tiled=True), 0, [])
+    out, at, done = (all_by_exchange(both, axis, 0), 0, [])
     for t, dim in zip(turned, dims):
         piece = out[:, at : at + t[0].size].reshape(-1, *t.shape[1:])
         done.append(jnp.moveaxis(piece, 0, dim))

time: 218 us -> 306 us (1.40)
  waiting for transfers between devices: 74.4 us -> 147 us
  blocking collectives: 0 us -> 14.9 us
  starting transfers between devices: 56.8 us -> 70.6 us
  between operations: 14.5 us -> 1.15 us
    all_to_all x1, waiting for transfers between devices: 11.2 us -> 107 us  [all_by_exchange(): blocks = lax.all_to_all(blocks, mesh_axis, split_axis=0, concat_axis=0)]
    all_gather x1 -> x0, waiting for transfers between devices: 26.7 us -> none  [turned_gather(): out, at, done = (lax.all_gather(both, axis, axis=0, tiled=True), 0, [])]
    all_to_all x0 -> x1, blocking collectives: none -> 14.9 us  [body(): lax.all_to_all(outgoing, 'resp', split_axis=0, concat_axis=2, tiled=True)[0]]
    all_to_all x1, starting transfers between devices: 8.03 us -> 22.2 us  [body(): lax.all_to_all(grad_prompt_rows[None].astype(jnp.bfloat16), 'resp', split...]
    unnamed x30 -> x40, local copies, waits for them, and re-layouts: 5.29 us -> 6.2 us
  transfers between devices with their start and end apart: 8 -> 7, of which waited for: 8 -> 7; matrix products, arithmetic and copies ran while one was open for 9% -> 5% of each run, Pallas kernels for 0% -> 0%
where the time goes in v1:
time: 306 us; the launch traced here: 305 us
  waiting for transfers between devices  147 us (48%)
  starting transfers between devices  70.6 us (23%)
  local copies, waits for them, and re-layouts  38.5 us (13%)
  other arithmetic  19.4 us (6%)
  blocking collectives  14.9 us (5%)
  matrix products  13.8 us (5%)
    all_to_all x1, waiting for transfers between devices, all_by_exchange(): blocks = lax.all_to_all(blocks, mesh_axis, split_axis=0, concat_axis=0)  107 us
    all_to_all x1, starting transfers between devices, body(): lax.all_to_all(grad_prompt_rows[None].astype(jnp.bfloat16), 'resp', split...  22.2 us
    all_to_all x1, starting transfers between devices, body(): lax.all_to_all(latent_share, 'resp', split_axis=1, concat_axis=0, tiled=T...  17.1 us
    all_to_all x1, blocking collectives, body(): lax.all_to_all(outgoing, 'resp', split_axis=0, concat_axis=2, tiled=True)[0]  14.9 us
    all_to_all x2, starting transfers between devices, sent_and_summed(): tiles = lax.all_to_all(split_up(array, dim, length), axis, 0, 0, tiled=True)  13.2 us
    sub x1, other arithmetic, attend(): grad_weights - inner  11.3 us
    slice x3, local copies, waits for them, and re-layouts, turned_gather(): piece = out[:, at:at + t[0].size].reshape(-1, *t.shape[1:])  10.5 us
    all_to_all x1, waiting for transfers between devices, body(): lax.all_to_all(summed.astype(jnp.bfloat16), 'resp', split_axis=0, concat_...  10.1 us
  transfers between devices with their start and end apart: 7, of which 7 were waited for; matrix products, arithmetic and copies ran while one was open for 5% of the time, Pallas kernels for 0%

profile of v1, /device:TPU:1, one launch (start us, length us, event | category | flops | bytes accessed | tf_op | source)
XLA Modules:
  0.0 305.2 jit_solution(1976460120917905606)
XLA Ops:
  0.7 0.9 copy-done
  1.6 0.8 copy.159
  2.3 17.1 %all-to-all-start.1 = ((bf16[1,128,72]{2,0,1:T(2,128)(2,1)}), bf16[1,128,72]{2,0,1:T(2,128)(2,1)S(1)}, u32[]{:S(2)}, u32[]{:S(2)}) async-start(bf16[1,128,72]{2,0,1:T(2,128)(2,1)} %copy.159), calls=%async_computation.1 | async-start | bytes 131072 | tf_op jit(solution)/shard_map/all_to_all | solution.py:129
  19.4 0.7 copy.118
  21.1 0.8 select_reduce_fusion.1
  22.1 8.5 %all-to-all-done.1 = bf16[1,128,72]{2,0,1:T(2,128)(2,1)S(1)} async-done(((bf16[1,128,72]{2,0,1:T(2,128)(2,1)}), bf16[1,128,72]{2,0,1:T(2,128)(2,1)S(1)}, u32[]{:S(2)}, u32[]{:S(2)}) %all-to-all-start.1) | async-done | bytes 18464 | tf_op jit(solution)/shard_map/all_to_all | solution.py:129
  30.6 0.7 gather_fusion
  31.5 14.9 %all_to_all.71 = bf16[64,2,2,72]{3,2,1,0:T(2,128)(2,1)S(1)} all-to-all(bf16[64,2,2,72]{3,2,1,0:T(2,128)(2,1)S(1)} %broadcast_select_fusion), channel_id=1, replica_groups=mesh['resp'=64,'head'=8] {'resp'}, dimensions={0} | all-to-all | bytes 73728 | tf_op jit(solution)/shard_map/all_to_all | solution.py:132
  46.6 0.8 broadcast_in_dim.82
  47.3 7.6 %all-to-all-start.3 = ((bf16[8,2,128,72]{2,3,1,0:T(8,128)(2,1)}), bf16[8,2,128,72]{2,3,1,0:T(8,128)(2,1)S(1)}, u32[]{:S(2)}, u32[]{:S(2)}) async-start(bf16[8,2,128,72]{2,3,1,0:T(8,128)(2,1)} %broadcast_in_dim.82), calls=%async_computation.3 | async-start | bytes 589824 | tf_op jit(solution)/shard_map/all_to_all | solution.py:34
  54.9 6.8 %all-to-all-done.3 = bf16[8,2,128,72]{2,3,1,0:T(8,128)(2,1)S(1)} async-done(((bf16[8,2,128,72]{2,3,1,0:T(8,128)(2,1)}), bf16[8,2,128,72]{2,3,1,0:T(8,128)(2,1)S(1)}, u32[]{:S(2)}, u32[]{:S(2)}) %all-to-all-start.3) | async-done | bytes 294944 | tf_op jit(solution)/shard_map/all_to_all | solution.py:34
  61.7 2.5 stack.2
  64.2 6.0 %all-to-all-start = ((bf16[64,8,4096]{2,1,0:T(8,128)(2,1)}), bf16[64,8,4096]{2,1,0:T(8,128)(2,1)}, u32[]{:S(2)}, u32[]{:S(2)}) async-start(bf16[64,8,4096]{2,1,0:T(8,128)(2,1)} %stack.2), calls=%async_computation | async-start | bytes 8388608 | tf_op jit(solution)/shard_map/all_to_all | solution.py:11
  70.2 1.1 reshape_reshape.6
  72.3 0.9 copy.160
  73.5 0.9 copy.127
  74.4 107.3 %all-to-all-done = bf16[64,8,4096]{2,1,0:T(8,128)(2,1)} async-done(((bf16[64,8,4096]{2,1,0:T(8,128)(2,1)}), bf16[64,8,4096]{2,1,0:T(8,128)(2,1)}, u32[]{:S(2)}, u32[]{:S(2)}) %all-to-all-start) | async-done | bytes 4194336 | tf_op jit(solution)/shard_map/all_to_all | solution.py:11
  181.6 4.8 %fusion.55 = (bf16[512,2048]{1,0:T(8,128)(2,1)}, bf16[512,2048]{1,0:T(8,128)(2,1)}) fusion(bf16[512,4096]{1,0:T(8,128)(2,1)} %bitcast.4), kind=kLoop, calls=%fused_computation.79 | loop fusion | bytes 8388608 | tf_op jit(solution)/shard_map/slice | solution.py:20
  186.4 2.9 copy.116
  189.3 2.4 copy.117
  191.7 2.9 copy.119
  194.6 1.7 fusion.66
  196.7 1.9 pad_maximum_fusion
  198.6 5.2 %fusion.56 = (f32[2,64,16]{2,1,0:T(8,128)S(1)}, f32[2,64,16,192]{3,2,1,0:T(8,128)}) fusion(pred[2,64,192]{2,1,0:T(8,128)(4,1)S(1)} %pad_add_fusion, bf16[2,64,16,576]{3,1,0,2:T(8,128)(2,1)} %pad_maximum_fusion, bf16[2,64,576]{2,1,0:T(8,128)(2,1)S(1)} %bitcast.135, bf16[2,128,576]{2,1,0:T(8,128)(2,1)} %copy.127), kind=kOutput, calls=%fused_computation.80 | convolution fusion | flops 455442624 | bytes 4407296 | tf_op jit(solution)/shard_map/vmap()/sub | solution.py:68
  203.8 2.0 fusion.54
  205.8 0.7 convolution_convert_fusion.1
  206.5 0.9 copy-done.2
  207.4 0.7 fusion.7
  208.8 0.7 fusion.22
  209.5 1.3 fusion.13
  211.1 11.3 %multiply_convert_fusion.1 = bf16[2,64,16,192]{3,2,1,0:T(8,128)(2,1)S(1)} fusion(f32[2,64,16,192]{3,2,1,0:T(8,128)S(1)} %fusion.13, f32[2,64,16,192]{3,2,1,0:T(8,128)S(1)} %copy-done.5, f32[2,64,16]{2,1,0:T(8,128)S(1)} %get-tuple-element.24), kind=kOutput, calls=%fused_computation.18 | output fusion | flops 2754751 | bytes 3940352 | tf_op jit(solution)/shard_map/vmap()/sub | solution.py:80
  222.3 0.9 fusion.28
  223.3 1.0 convolution_convert_fusion
  224.3 1.8 slice.48
  227.7 0.9 copy.191
  228.9 0.8 copy.143
  229.6 7.4 %all-to-all-start.5 = ((bf16[8,2,128,72]{2,3,1,0:T(8,128)(2,1)}), bf16[8,2,128,72]{2,3,1,0:T(8,128)(2,1)S(1)}, u32[]{:S(2)}, u32[]{:S(2)}) async-start(bf16[8,2,128,72]{2,3,1,0:T(8,128)(2,1)} %copy.143), calls=%async_computation.5 | async-start | bytes 589824 | tf_op jit(solution)/shard_map/all_to_all | solution.py:48
  237.3 0.9 copy.140
  238.2 2.8 copy.133
  242.2 1.6 all-to-all-done.5
  243.9 0.7 copy.145
  244.6 22.2 %all-to-all-start.6 = ((bf16[1,2,128,72]{3,1,0,2:T(2,128)(2,1)}), bf16[1,2,128,72]{3,1,0,2:T(2,128)(2,1)S(1)}, u32[]{:S(2)}, u32[]{:S(2)}) async-start(bf16[1,2,128,72]{3,1,0,2:T(2,128)(2,1)} %copy.145), calls=%async_computation.6 | async-start | bytes 131072 | tf_op jit(solution)/shard_map/all_to_all | solution.py:158
  267.7 2.0 convert_element_type.102
  269.7 8.2 %all-to-all-done.6 = bf16[1,2,128,72]{3,1,0,2:T(2,128)(2,1)S(1)} async-done(((bf16[1,2,128,72]{3,1,0,2:T(2,128)(2,1)}), bf16[1,2,128,72]{3,1,0,2:T(2,128)(2,1)S(1)}, u32[]{:S(2)}, u32[]{:S(2)}) %all-to-all-start.6) | async-done | bytes 36896 | tf_op jit(solution)/shard_map/all_to_all | solution.py:158
  277.9 5.8 %all-to-all-start.4 = ((bf16[8,128,72]{1,2,0:T(8,128)(2,1)}), bf16[8,128,72]{1,2,0:T(8,128)(2,1)S(1)}, u32[]{:S(2)}, u32[]{:S(2)}) async-start(bf16[8,128,72]{1,2,0:T(8,128)(2,1)} %copy.140), calls=%async_computation.4 | async-start | bytes 294912 | tf_op jit(solution)/shard_map/all_to_all | solution.py:48
  284.8 4.3 %all-to-all-done.4 = bf16[8,128,72]{1,2,0:T(8,128)(2,1)S(1)} async-done(((bf16[8,128,72]{1,2,0:T(8,128)(2,1)}), bf16[8,128,72]{1,2,0:T(8,128)(2,1)S(1)}, u32[]{:S(2)}, u32[]{:S(2)}) %all-to-all-start.4) | async-done | bytes 147488 | tf_op jit(solution)/shard_map/all_to_all | solution.py:48
  289.1 4.6 %all-to-all-start.7 = ((bf16[64,2,72]{2,1,0:T(2,128)(2,1)}), bf16[64,2,72]{2,1,0:T(2,128)(2,1)S(1)}, u32[]{:S(2)}, u32[]{:S(2)}) async-start(bf16[64,2,72]{2,1,0:T(2,128)(2,1)} %copy.149), calls=%async_computation.7 | async-start | bytes 65536 | tf_op jit(solution)/shard_map/all_to_all | solution.py:167
  294.4 10.1 %all-to-all-done.7 = bf16[64,2,72]{2,1,0:T(2,128)(2,1)S(1)} async-done(((bf16[64,2,72]{2,1,0:T(2,128)(2,1)}), bf16[64,2,72]{2,1,0:T(2,128)(2,1)S(1)}, u32[]{:S(2)}, u32[]{:S(2)}) %all-to-all-start.7) | async-done | bytes 18464 | tf_op jit(solution)/shard_map/all_to_all | solution.py:167
  (88 shorter events, 10.6 us)
Async XLA Ops:
  0.6 0.9 copy-start
  0.6 54.3 %copy-start.13 = (bf16[16,8,128]{2,1,0:T(8,128)(2,1)S(1)}, bf16[16,8,128]{2,1,0:T(8,128)(2,1)}, u32[]{:S(2)}) copy-start(bf16[16,8,128]{2,1,0:T(8,128)(2,1)} %param.14) | copy-start | bytes 98308
  0.7 54.2 %copy-start.14 = (bf16[16,128,8]{1,2,0:T(8,128)(2,1)S(1)}, bf16[16,128,8]{1,2,0:T(8,128)(2,1)}, u32[]{:S(2)}) copy-start(bf16[16,128,8]{1,2,0:T(8,128)(2,1)} %param.13) | copy-start | bytes 98308
  2.3 28.3 %all-to-all-start.1 = ((bf16[1,128,72]{2,0,1:T(2,128)(2,1)}), bf16[1,128,72]{2,0,1:T(2,128)(2,1)S(1)}, u32[]{:S(2)}, u32[]{:S(2)}) async-start(bf16[1,128,72]{2,0,1:T(2,128)(2,1)} %copy.159), calls=%async_computation.1 | async-start | bytes 131072 | tf_op jit(solution)/shard_map/all_to_all | solution.py:129
  47.3 14.3 %all-to-all-start.3 = ((bf16[8,2,128,72]{2,3,1,0:T(8,128)(2,1)}), bf16[8,2,128,72]{2,3,1,0:T(8,128)(2,1)S(1)}, u32[]{:S(2)}, u32[]{:S(2)}) async-start(bf16[8,2,128,72]{2,3,1,0:T(8,128)(2,1)} %broadcast_in_dim.82), calls=%async_computation.3 | async-start | bytes 589824 | tf_op jit(solution)/shard_map/all_to_all | solution.py:34
  61.7 2.5 copy-start.8
  64.2 6.0 %copy-start.10 = (bf16[128,3072]{1,0:T(8,128)(2,1)S(1)}, bf16[128,3072]{1,0:T(8,128)(2,1)}, u32[]{:S(2)}) copy-start(bf16[128,3072]{1,0:T(8,128)(2,1)} %param.10) | copy-start | bytes 2359300
  64.2 117.5 %all-to-all-start = ((bf16[64,8,4096]{2,1,0:T(8,128)(2,1)}), bf16[64,8,4096]{2,1,0:T(8,128)(2,1)}, u32[]{:S(2)}, u32[]{:S(2)}) async-start(bf16[64,8,4096]{2,1,0:T(8,128)(2,1)} %stack.2), calls=%async_computation | async-start | bytes 8388608 | tf_op jit(solution)/shard_map/all_to_all | solution.py:11
  70.2 1.4 copy-start.15
  70.2 1.5 copy-start.12
  70.2 1.7 copy-start.11
  71.9 1.6 copy-start.9
  203.8 2.0 copy-start.6
  205.8 1.6 copy-start.2
  209.5 1.6 copy-start.5
  211.1 11.3 %copy-start.4 = (bf16[2,64,16,576]{3,1,0,2:T(8,128)(2,1)S(1)}, bf16[2,64,16,576]{3,1,0,2:T(8,128)(2,1)}, u32[]{:S(2)}) copy-start(bf16[2,64,16,576]{3,1,0,2:T(8,128)(2,1)} %pad_maximum_fusion) | copy-start | bytes 7077892
  223.3 1.0 copy-start.7
  224.3 2.2 copy-start.3
  227.2 1.5 slice-start.2
  227.4 9.7 %slice-start.1 = ((bf16[2,192,576]{2,1,0:T(8,128)(2,1)}), bf16[2,64,576]{2,1,0:T(8,128)(2,1)S(1)}, s32[]{:S(2)}) async-start(bf16[2,192,576]{2,1,0:T(8,128)(2,1)} %copy-done.7), calls=%async_computation.9 | async-start | bytes 327680 | tf_op jit(solution)/shard_map/slice | solution.py:152
  229.6 14.2 %all-to-all-start.5 = ((bf16[8,2,128,72]{2,3,1,0:T(8,128)(2,1)}), bf16[8,2,128,72]{2,3,1,0:T(8,128)(2,1)S(1)}, u32[]{:S(2)}, u32[]{:S(2)}) async-start(bf16[8,2,128,72]{2,3,1,0:T(8,128)(2,1)} %copy.143), calls=%async_computation.5 | async-start | bytes 589824 | tf_op jit(solution)/shard_map/all_to_all | solution.py:48
  240.9 1.0 slice-start
  244.6 33.3 %all-to-all-start.6 = ((bf16[1,2,128,72]{3,1,0,2:T(2,128)(2,1)}), bf16[1,2,128,72]{3,1,0,2:T(2,128)(2,1)S(1)}, u32[]{:S(2)}, u32[]{:S(2)}) async-start(bf16[1,2,128,72]{3,1,0,2:T(2,128)(2,1)} %copy.145), calls=%async_computation.6 | async-start | bytes 131072 | tf_op jit(solution)/shard_map/all_to_all | solution.py:158
  267.1 38.2 %copy-start.1 = (bf16[1,128,576]{1,2,0:T(8,128)(2,1)S(1)}, bf16[1,128,576]{1,2,0:T(8,128)(2,1)}, u32[]{:S(2)}) copy-start(bf16[1,128,576]{1,2,0:T(8,128)(2,1)} %param.12) | copy-start | bytes 442372
  277.9 11.2 %all-to-all-start.4 = ((bf16[8,128,72]{1,2,0:T(8,128)(2,1)}), bf16[8,128,72]{1,2,0:T(8,128)(2,1)S(1)}, u32[]{:S(2)}, u32[]{:S(2)}) async-start(bf16[8,128,72]{1,2,0:T(8,128)(2,1)} %copy.140), calls=%async_computation.4 | async-start | bytes 294912 | tf_op jit(solution)/shard_map/all_to_all | solution.py:48
  289.1 15.4 %all-to-all-start.7 = ((bf16[64,2,72]{2,1,0:T(2,128)(2,1)}), bf16[64,2,72]{2,1,0:T(2,128)(2,1)S(1)}, u32[]{:S(2)}, u32[]{:S(2)}) async-start(bf16[64,2,72]{2,1,0:T(2,128)(2,1)} %copy.149), calls=%async_computation.7 | async-start | bytes 65536 | tf_op jit(solution)/shard_map/all_to_all | solution.py:167
